TPU v7x, 256 devices: a whole 4x4x8 slice. The times are simulated.
256 devices in a mesh: blk: 8 (over x_hi, y), tok: 32 (over x_lo, z, core).
Axes of the slice: x: 4 (x_hi: 2, x_lo: 2; x = x_hi * 2 + x_lo), y: 4, z: 8, core: 2. Of those that a mesh axis runs over, the one named last changes fastest.
Arguments:
- states: bfloat16 [1024, 3584], P('tok'), may hold values from -30 to 30
- head: bfloat16 [3584, 262144], P(None, ('blk', 'tok')), may hold values from -0.2 to 0.2
- targets: int32 [1024], P('tok'), may hold values from 0 to 262143
- ref_loss: float32 [1024], P('tok'), may hold values from 0 to 8
- seq_ids: int32 [1024], P('tok'), may hold values from 0 to 511, never falling along the last dimension, each value on 1 to 4 neighbouring positions
Outputs:
- excess: float32 [1024], P('tok')
- seq_score: float32 [512], replicated
Inputs may be any that keep to these rules, and one draw needn't show every extreme that they name: `seq_ids`: sequence numbers never fall along the tokens; every number from 0 to 511 occurs, on 1 to 4 consecutive tokens.
All inputs are finite; a program needn't handle non-finite values.
Results may differ from a plain program's by a relative error of at most 0.0003.
Values may be sent and summed in bfloat16 or wider, within the bound.
No kernel may reach another device: no remote copies, remote signals or barrier semaphores. Data moves between devices by JAX's collectives and lax.ppermute only.
A program may use at most 64 MiB of HBM per device.

v0:
```python
import jax
import jax.numpy as jnp
from jax import lax
from jax.sharding import Mesh
from jax.sharding import PartitionSpec as P

TOK = ("tok_0", "tok_1", "tok_2")
BLK = ("blk_0", "blk_1")
BLK_TOK = ("blk_0", "blk_1", "tok_0", "tok_1", "tok_2")
very_low = -1e30


def all_in_one(value, axis):
    leaves = jax.tree.leaves(value)
    turns = sorted(range(len(leaves)), key=lambda k: -leaves[k].size)
    width = (1, *leaves[turns[0]].shape)[-1]
    lines = [
        jnp.pad(leaves[k].reshape(-1), (0, -leaves[k].size % width)).reshape(-1, width)
        for k in turns
    ]
    both, at, found = (lax.all_gather(jnp.concatenate(lines), axis), 0, {})
    for k, line in zip(turns, lines):
        section = both[:, at : at + len(line)].reshape(len(both), -1)
        found[k] = section[:, : leaves[k].size].reshape(-1, *leaves[k].shape)
        at += len(line)
    numbers = iter(range(len(leaves)))
    return jax.tree.map(lambda _: found[next(numbers)], value)


def merged_by_axis(value, axes, combine):
    for axis in axes:
        pieces = all_in_one(value, axis)
        value = jax.tree.map(lambda part: part[0], pieces)
        for k in range(1, lax.axis_size(axis)):
            value = combine(value, jax.tree.map(lambda part: part[k], pieces))
    return value


def copy_for_each(value, axis):
    devices = lax.axis_size(axis)
    return lax.all_to_all(
        jnp.broadcast_to(value[None], (devices, *value.shape)), axis, 0, 0, tiled=True
    )


def of_everyone(value, axis):
    return copy_for_each(value, axis).sum(axis=0)


def packed_total(arrays, axis):
    vector, at, gathered = (jnp.concatenate([a.reshape(-1) for a in arrays]), 0, [])
    so_far = of_everyone(vector, axis)
    for a in arrays:
        gathered.append(so_far[at : at + a.size].reshape(a.shape))
        at += a.size
    return tuple(gathered)


def absorb(highest, scaled, picked, token_rows, target_ids, head, first_col):
    logits = jnp.dot(token_rows, head, preferred_element_type=jnp.float32)
    new_high = jnp.maximum(highest, jnp.max(logits, axis=1))
    scaled = jnp.sum(jnp.exp(logits - new_high[:, None]), axis=1)
    columns = first_col + lax.iota(jnp.int32, head.shape[1])
    hits = columns[None, :] == target_ids[:, None]
    picked = jnp.sum(jnp.where(hits, logits, 0.0), axis=1)
    return (new_high, scaled, picked)


def combine_stats(left, right):
    left_high, left_scaled, left_picked = left
    right_high, right_scaled, right_picked = right
    highest = jnp.maximum(left_high, right_high)
    scaled = left_scaled * jnp.exp(left_high - highest) + right_scaled * jnp.exp(
        right_high - highest
    )
    return (highest, scaled, left_picked + right_picked)


def on_device(states, head, targets, ref_loss, seq_ids):
    cycle_size = lax.axis_size(TOK)
    first_col = (lax.axis_index(BLK) * cycle_size + lax.axis_index(TOK)) * head.shape[1]
    local = states.shape[0]
    total = local * cycle_size
    begin = (
        jnp.full((total,), very_low, jnp.float32),
        jnp.zeros((total,), jnp.float32),
        jnp.zeros((total,), jnp.float32),
    )
    token_rows = lax.all_gather(states, TOK, axis=0, tiled=True)
    target_ids = lax.all_gather(targets, TOK, axis=0, tiled=True)
    current = [member for member in begin]
    updated = absorb(current[0], current[1], current[2], token_rows, target_ids, head, first_col)
    highest, scaled, picked = tuple((fresh for fresh in updated))
    highest, scaled, picked = merged_by_axis((highest, scaled, picked), BLK_TOK, combine_stats)
    own_start = lax.axis_index(TOK) * local
    highest = lax.dynamic_slice_in_dim(highest, own_start, local)
    scaled = lax.dynamic_slice_in_dim(scaled, own_start, local)
    picked = lax.dynamic_slice_in_dim(picked, own_start, local)
    excess = highest + jnp.log(scaled) - picked - ref_loss
    seq_count = local * cycle_size // 2
    member = (seq_ids[:, None] == lax.iota(jnp.int32, seq_count)[None, :]).astype(jnp.float32)
    totals = jnp.dot(excess, member, precision=lax.Precision.HIGHEST)
    counts = jnp.sum(member, axis=0)
    totals, counts = packed_total((totals, counts), TOK)
    return (excess, totals / counts)


def solution(mesh):
    torus = Mesh(mesh.devices.reshape(2, 4, 2, 8, 2), ("blk_0", "blk_1", "tok_0", "tok_1", "tok_2"))
    return jax.shard_map(
        on_device,
        mesh=torus,
        in_specs=(P(TOK, None), P(None, BLK_TOK), P(TOK), P(TOK), P(TOK)),
        out_specs=(P(TOK), P()),
        check_vma=False,
    )
```

profile of v0, /device:TPU:1, one launch (start us, length us, event | category | flops | bytes accessed | tf_op | source)
XLA Modules:
  0.0 171.1 jit_solution(2445208449246371563)
XLA Ops:
  7.2 0.0 all-gather.12.cloned.1.call-start
  7.2 0.7 all-gather.12.cloned.1.call-update
  7.9 1.3 dynamic-slice.1
  9.8 0.9 dynamic-update-slice
  10.7 17.2 %all-reduce = s32[1024]{0:T(1024)S(1)} all-reduce(s32[1024]{0:T(1024)S(1)} %dynamic-update-slice), channel_id=1, replica_groups=mesh['blk_0'=2,'blk_1'=4,'tok_0'=2,'tok_1'=8,'tok_2'=2] {'tok_0','tok_1'..., use_global_device_ids=true, to_apply=%add | all-reduce | flops 1024 | bytes 8192
  27.9 0.7 convert_reduce_fusion
  28.7 56.3 %all-gather.12.cloned.1.call-done = bf16[1024,3584]{1,0:T(8,128)(2,1)} async-done(((bf16[32,3584]{1,0:T(8,128)(2,1)}), bf16[1024,3584]{1,0:T(8,128)(2,1)}) %all-gather.12.cloned.1.call-update) | async-done | bytes 7340048 | tf_op jit(solution)/shard_map/all_gather | solution.py:89
  84.9 12.2 %fusion.63 = (f32[1024]{0:T(1024)S(1)}, f32[1024,1024]{0,1:T(8,128)S(1)}) fusion(bf16[1024,3584]{1,0:T(8,128)(2,1)} %all-gather.12.cloned.1.call-done, bf16[3584,1024]{1,0:T(8,128)(2,1)} %param.6), kind=kOutput, calls=%fused_computation.118 | convolution fusion | flops 7517240320 | bytes 18878464 | tf_op jit(solution)/shard_map/dot_general | solution.py:60
  97.2 0.0 copy-start
  97.2 0.0 copy-start.1
  97.2 1.4 exponential_reduce_fusion
  98.7 4.8 %all-gather.5 = f32[2,3,1024]{2,1,0:T(4,128)S(1)} all-gather(f32[1,3,1024]{2,1,0:T(4,128)S(1)} %maximum_bitcast_fusion), channel_id=2, replica_groups=mesh['blk_0'=2,'blk_1'=4,'tok_0'=2,'tok_1'=8,'tok_2'=2] {'blk_0'}, dimensions={0}, use_global_device_ids=true | all-gather | bytes 36864 | tf_op jit(solution)/shard_map/all_gather | solution.py:21
  103.5 9.3 %all-gather.6 = f32[4,3,1024]{2,1,0:T(4,128)S(1)} all-gather(f32[1,3,1024]{2,1,0:T(4,128)S(1)} %maximum_bitcast_fusion.1), channel_id=3, replica_groups=mesh['blk_0'=2,'blk_1'=4,'tok_0'=2,'tok_1'=8,'tok_2'=2] {'blk_1'}, dimensions={0}, use_global_device_ids=true | all-gather | bytes 61440 | tf_op jit(solution)/shard_map/all_gather | solution.py:21
  112.8 0.1 fusion.30
  112.9 3.5 %all-gather.7 = f32[2,3,1024]{2,1,0:T(4,128)S(1)} all-gather(f32[1,3,1024]{2,1,0:T(4,128)S(1)} %maximum_bitcast_fusion.2), channel_id=4, replica_groups=mesh['blk_0'=2,'blk_1'=4,'tok_0'=2,'tok_1'=8,'tok_2'=2] {'tok_0'}, dimensions={0}, use_global_device_ids=true | all-gather | bytes 36864 | tf_op jit(solution)/shard_map/all_gather | solution.py:21
  116.5 18.3 %all-gather.8 = f32[8,3,1024]{2,1,0:T(4,128)S(1)} all-gather(f32[1,3,1024]{2,1,0:T(4,128)S(1)} %maximum_bitcast_fusion.3), channel_id=5, replica_groups=mesh['blk_0'=2,'blk_1'=4,'tok_0'=2,'tok_1'=8,'tok_2'=2] {'tok_1'}, dimensions={0}, use_global_device_ids=true | all-gather | bytes 110592 | tf_op jit(solution)/shard_map/all_gather | solution.py:21
  134.8 0.1 fusion.4
  135.0 13.0 %all-gather.9 = f32[2,3,1024]{2,1,0:T(4,128)S(1)} all-gather(f32[1,3,1024]{2,1,0:T(4,128)S(1)} %maximum_bitcast_fusion.4), channel_id=6, replica_groups=mesh['blk_0'=2,'blk_1'=4,'tok_0'=2,'tok_1'=8,'tok_2'=2] {'tok_2'}, dimensions={0}, use_global_device_ids=true | all-gather | bytes 36864 | tf_op jit(solution)/shard_map/all_gather | solution.py:21
  148.0 0.0 copy-done
  148.0 0.1 fusion.56
  148.1 0.0 copy-done.1
  148.1 0.0 copy-start.2
  148.1 0.2 fusion
  148.3 0.1 broadcast_in_dim.10
  148.4 15.2 %all_to_all.6 = f32[32,1,1024]{2,1,0:T(1,128)S(1)} all-to-all(f32[32,1,1024]{2,1,0:T(1,128)S(1)} %broadcast_in_dim.10), channel_id=1, replica_groups=mesh['blk_0'=2,'blk_1'=4,'tok_0'=2,'tok_1'=8,'tok_2'=2] {'tok_0','tok_1'..., dimensions={0} | all-to-all | bytes 262144 | tf_op jit(solution)/shard_map/all_to_all | solution.py:41
  163.6 0.1 reduce_sum.39
  163.7 0.6 slice_divide_fusion
  164.2 0.0 copy-done.2
  (17 shorter events, 0.3 us)
Async XLA Ops:
  7.2 77.8 %all-gather.12.cloned.1.call-start = ((), (), s32[]{:S(2)}) async-start(), calls=%async_computation.1 | async-start | bytes 7569408 | tf_op jit(solution)/shard_map/all_gather | solution.py:89
  97.2 50.8 %copy-start = (f32[32]{0:T(128)S(1)}, f32[32]{0:T(128)}, u32[]{:S(2)}) copy-start(f32[32]{0:T(128)} %param.8) | copy-start | bytes 388
  97.2 50.9 %copy-start.1 = (s32[32]{0:T(128)S(1)}, s32[32]{0:T(128)}, u32[]{:S(2)}) copy-start(s32[32]{0:T(128)} %param.9) | copy-start | bytes 388
  148.1 16.2 %copy-start.2 = (f32[32]{0:T(128)}, f32[32]{0:T(128)S(1)}, u32[]{:S(2)}) copy-start(f32[32]{0:T(128)S(1)} %fusion.56) | copy-start | bytes 388
Sparse Core Ops, SparseCore 0:
  9.8 75.0 all-gather.11
where the time goes:
time: 171 us
  blocking collectives  81.3 us (48%)
  waiting for transfers between devices  57 us (33%)
  between operations  14.8 us (9%)
  matrix products  12.4 us (7%)
  other arithmetic  3.31 us (2%)
  local copies, waits for them, and re-layouts  2.24 us (1%)
    all_gather x1, waiting for transfers between devices, on_device(): token_rows = lax.all_gather(states, TOK, axis=0, tiled=True)  56.3 us
    all_gather x5, blocking collectives, all_in_one(): both, at, found = (lax.all_gather(jnp.concatenate(lines), axis), 0, {})  48.9 us
    unnamed x1, blocking collectives  17.2 us
    all_to_all x1, blocking collectives, copy_for_each(): lax.all_to_all(jnp.broadcast_to(value[None], (devices, *value.shape)), ax...  15.2 us
    dot_general x1, matrix products, absorb(): logits = jnp.dot(token_rows, head, preferred_element_type=jnp.float32)  12.2 us
  transfers between devices with their start and end apart: 1, of which 1 were waited for; matrix products, arithmetic and copies ran while one was open for 2% of the time, Pallas kernels for 0%

commit v1 on v0

--- a/solution.py
+++ b/solution.py
@@ -86,7 +86,9 @@
         jnp.zeros((total,), jnp.float32),
         jnp.zeros((total,), jnp.float32),
     )
-    token_rows = lax.all_gather(states, TOK, axis=0, tiled=True)
+    token_rows = jnp.concatenate(
+        lax.all_to_all(jnp.stack([states] * lax.axis_size(TOK)), TOK, 0, 0), axis=0
+    )
     target_ids = lax.all_gather(targets, TOK, axis=0, tiled=True)
     current = [member for member in begin]
     updated = absorb(current[0], current[1], current[2], token_rows, target_ids, head, first_col)

time: 171 us -> 267 us (1.56)
  blocking collectives: 81.3 us -> 233 us
  waiting for transfers between devices: 57 us -> 0.01 us
  between operations: 14.8 us -> 1.48 us
  starting transfers between devices: 0.04 us -> 11.2 us
  local copies, waits for them, and re-layouts: 2.24 us -> 5.74 us
    unnamed x1, blocking collectives: 17.2 us -> 169 us
    all_gather x1 -> x0, waiting for transfers between devices: 56.3 us -> none  [on_device(): token_rows = lax.all_gather(states, TOK, axis=0, tiled=True)]
    all_to_all x0 -> x1, starting transfers between devices: none -> 11.2 us  [on_device(): lax.all_to_all(jnp.stack([states] * lax.axis_size(TOK)), TOK, 0, 0)]
    another operation x0 -> x1, local copies, waits for them, and re-layouts: none -> 4.79 us  [on_device(): jnp.stack([states] * lax.axis_size(TOK))]
    all_gather x5, blocking collectives: 48.9 us -> 51.9 us  [all_in_one(): both, at, found = (lax.all_gather(jnp.concatenate(lines), axis), 0, {})]
    all_to_all x1, blocking collectives: 15.2 us -> 12.4 us  [copy_for_each(): lax.all_to_all(jnp.broadcast_to(value[None], (devices, *value.shape)), ax...]
  transfers between devices with their start and end apart: 1 -> 1, of which waited for: 1 -> 0; matrix products, arithmetic and copies ran while one was open for 2% -> 0% of each run, Pallas kernels for 0% -> 0%
where the time goes in v1:
time: 267 us
  blocking collectives  233 us (87%)
  matrix products  12.5 us (5%)
  starting transfers between devices  11.2 us (4%)
  local copies, waits for them, and re-layouts  5.74 us (2%)
    unnamed x1, blocking collectives  169 us
    all_gather x5, blocking collectives, all_in_one(): both, at, found = (lax.all_gather(jnp.concatenate(lines), axis), 0, {})  51.9 us
    all_to_all x1, blocking collectives, copy_for_each(): lax.all_to_all(jnp.broadcast_to(value[None], (devices, *value.shape)), ax...  12.4 us
    dot_general x1, matrix products, absorb(): logits = jnp.dot(token_rows, head, preferred_element_type=jnp.float32)  12.3 us
    all_to_all x1, starting transfers between devices, on_device(): lax.all_to_all(jnp.stack([states] * lax.axis_size(TOK)), TOK, 0, 0)  11.2 us
  transfers between devices with their start and end apart: 1, of which 0 were waited for; matrix products, arithmetic and copies ran while one was open for 0% of the time, Pallas kernels for 0%

profile of v1, /device:TPU:1, one launch (start us, length us, event | category | flops | bytes accessed | tf_op | source)
XLA Modules:
  0.0 266.9 jit_solution(15062294571861555254)
XLA Ops:
  0.6 4.8 %stack.2 = bf16[32,32,3584]{2,1,0:T(8,128)(2,1)} broadcast(bf16[32,3584]{1,0:T(8,128)(2,1)} %param.5), dimensions={1,2} | broadcast | bytes 7569408 | tf_op jit(solution)/shard_map/stack | solution.py:90
  5.4 0.0 copy-start.4
  5.4 0.0 copy-start.3
  5.4 0.0 copy-start.1
  5.4 11.2 %all-to-all-start = ((bf16[32,32,3584]{2,1,0:T(8,128)(2,1)}), bf16[32,32,3584]{2,1,0:T(8,128)(2,1)}, u32[]{:S(2)}, u32[]{:S(2)}) async-start(bf16[32,32,3584]{2,1,0:T(8,128)(2,1)} %stack.2), calls=%async_computation | async-start | bytes 14680064 | tf_op jit(solution)/shard_map/all_to_all | solution.py:90
  16.7 0.0 copy-done.4
  16.7 0.6 dynamic-slice.1
  17.9 0.0 copy-done.3
  17.9 0.2 dynamic-update-slice
  18.2 169.0 %all-reduce = s32[1024]{0:T(1024)S(1)} all-reduce(s32[1024]{0:T(1024)S(1)} %dynamic-update-slice), channel_id=1, replica_groups=mesh['blk_0'=2,'blk_1'=4,'tok_0'=2,'tok_1'=8,'tok_2'=2] {'tok_0','tok_1'..., use_global_device_ids=true, to_apply=%add | all-reduce | flops 1024 | bytes 8192
  187.2 0.0 copy-done.1
  187.2 0.1 convert_reduce_fusion
  187.3 0.0 all-to-all-done
  187.3 12.3 %fusion.63 = (f32[1024]{0:T(1024)S(1)}, f32[1024,1024]{0,1:T(8,128)S(1)}) fusion(bf16[1024,3584]{1,0:T(8,128)(2,1)} %bitcast, bf16[3584,1024]{1,0:T(8,128)(2,1)} %param.6), kind=kOutput, calls=%fused_computation.118 | convolution fusion | flops 7517240320 | bytes 18878464 | tf_op jit(solution)/shard_map/dot_general | solution.py:60
  199.6 0.0 copy-start
  199.6 1.4 exponential_reduce_fusion
  201.0 4.8 %all-gather.5 = f32[2,3,1024]{2,1,0:T(4,128)S(1)} all-gather(f32[1,3,1024]{2,1,0:T(4,128)S(1)} %maximum_bitcast_fusion), channel_id=2, replica_groups=mesh['blk_0'=2,'blk_1'=4,'tok_0'=2,'tok_1'=8,'tok_2'=2] {'blk_0'}, dimensions={0}, use_global_device_ids=true | all-gather | bytes 36864 | tf_op jit(solution)/shard_map/all_gather | solution.py:21
  205.8 9.5 %all-gather.6 = f32[4,3,1024]{2,1,0:T(4,128)S(1)} all-gather(f32[1,3,1024]{2,1,0:T(4,128)S(1)} %maximum_bitcast_fusion.1), channel_id=3, replica_groups=mesh['blk_0'=2,'blk_1'=4,'tok_0'=2,'tok_1'=8,'tok_2'=2] {'blk_1'}, dimensions={0}, use_global_device_ids=true | all-gather | bytes 61440 | tf_op jit(solution)/shard_map/all_gather | solution.py:21
  215.4 0.1 fusion.30
  215.4 3.3 %all-gather.7 = f32[2,3,1024]{2,1,0:T(4,128)S(1)} all-gather(f32[1,3,1024]{2,1,0:T(4,128)S(1)} %maximum_bitcast_fusion.2), channel_id=4, replica_groups=mesh['blk_0'=2,'blk_1'=4,'tok_0'=2,'tok_1'=8,'tok_2'=2] {'tok_0'}, dimensions={0}, use_global_device_ids=true | all-gather | bytes 36864 | tf_op jit(solution)/shard_map/all_gather | solution.py:21
  218.8 18.2 %all-gather.8 = f32[8,3,1024]{2,1,0:T(4,128)S(1)} all-gather(f32[1,3,1024]{2,1,0:T(4,128)S(1)} %maximum_bitcast_fusion.3), channel_id=5, replica_groups=mesh['blk_0'=2,'blk_1'=4,'tok_0'=2,'tok_1'=8,'tok_2'=2] {'tok_1'}, dimensions={0}, use_global_device_ids=true | all-gather | bytes 110592 | tf_op jit(solution)/shard_map/all_gather | solution.py:21
  237.0 0.1 fusion.4
  237.2 16.2 %all-gather.9 = f32[2,3,1024]{2,1,0:T(4,128)S(1)} all-gather(f32[1,3,1024]{2,1,0:T(4,128)S(1)} %maximum_bitcast_fusion.4), channel_id=6, replica_groups=mesh['blk_0'=2,'blk_1'=4,'tok_0'=2,'tok_1'=8,'tok_2'=2] {'tok_2'}, dimensions={0}, use_global_device_ids=true | all-gather | bytes 36864 | tf_op jit(solution)/shard_map/all_gather | solution.py:21
  253.4 0.0 copy-done
  253.4 0.1 fusion.56
  253.5 0.0 copy-start.2
  253.5 0.2 fusion
  253.7 0.1 broadcast_in_dim.10
  253.8 12.4 %all_to_all.11 = f32[32,1,1024]{2,1,0:T(1,128)S(1)} all-to-all(f32[32,1,1024]{2,1,0:T(1,128)S(1)} %broadcast_in_dim.10), channel_id=1, replica_groups=mesh['blk_0'=2,'blk_1'=4,'tok_0'=2,'tok_1'=8,'tok_2'=2] {'tok_0','tok_1'..., dimensions={0} | all-to-all | bytes 262144 | tf_op jit(solution)/shard_map/all_to_all | solution.py:41
  266.2 0.1 reduce_sum.39
  266.3 0.6 slice_divide_fusion
  266.9 0.0 copy-done.2
  (17 shorter events, 0.3 us)
Async XLA Ops:
  5.4 11.2 %copy-start.4 = (u32[256]{0:T(256)S(1)}, u32[256]{0:T(256)}, u32[]{:S(2)}) copy-start(u32[256]{0:T(256)} %constant.42) | copy-start | bytes 3076
  5.4 12.5 %copy-start.3 = (s32[32]{0:T(128)S(1)}, s32[32]{0:T(128)}, u32[]{:S(2)}) copy-start(s32[32]{0:T(128)} %param.7) | copy-start | bytes 388
  5.4 181.8 %copy-start.1 = (s32[32]{0:T(128)S(1)}, s32[32]{0:T(128)}, u32[]{:S(2)}) copy-start(s32[32]{0:T(128)} %param.9) | copy-start | bytes 388
  5.4 181.9 %all-to-all-start = ((bf16[32,32,3584]{2,1,0:T(8,128)(2,1)}), bf16[32,32,3584]{2,1,0:T(8,128)(2,1)}, u32[]{:S(2)}, u32[]{:S(2)}) async-start(bf16[32,32,3584]{2,1,0:T(8,128)(2,1)} %stack.2), calls=%async_computation | async-start | bytes 14680064 | tf_op jit(solution)/shard_map/all_to_all | solution.py:90
  199.6 53.8 %copy-start = (f32[32]{0:T(128)S(1)}, f32[32]{0:T(128)}, u32[]{:S(2)}) copy-start(f32[32]{0:T(128)} %param.8) | copy-start | bytes 388
  253.5 13.4 %copy-start.2 = (f32[32]{0:T(128)}, f32[32]{0:T(128)S(1)}, u32[]{:S(2)}) copy-start(f32[32]{0:T(128)S(1)} %fusion.56) | copy-start | bytes 388
